TPU v7x, 8 devices: a whole 2x2x1 slice. The times are simulated.
8 devices in a mesh: dp: 1 (over z), vp: 2 (over y), tp: 4 (over x, core).
Axes of the slice: x: 2, y: 2, z: 1, core: 2. Of those that a mesh axis runs over, the one named last changes fastest.
Arguments:
- hidden: bfloat16 [16, 1024], P('dp', 'tp')
- lnf_gain: float32 [1024], P('tp')
- lnf_bias: float32 [1024], P('tp')
- emb_table: bfloat16 [250880, 1024], P('vp', 'tp')
- next_tok: int32 [16], P('dp')
- eln_gain: float32 [1024], P('tp')
- eln_bias: float32 [1024], P('tp')
Outputs:
- output 1: float32 [16, 250880], P('dp', ('vp', 'tp'))
- output 2: float32 [16], P('dp')
- output 3: bfloat16 [16, 1024], P('dp', 'tp')
All inputs are finite; a program needn't handle non-finite values.
Results may differ from a plain program's by a relative error of at most 0.001.
Values sent between devices are 32-bit elements.
A program may use at most 1 GiB of HBM per device.

v0:
```python
import jax
import jax.numpy as jnp
from jax import lax
from jax.sharding import PartitionSpec as P

NORM_EPS = 1e-5


def norm_shard(rows_in, norm_gain, norm_bias, full_width):
    rows_f32 = rows_in.astype(jnp.float32)
    row_sums = jnp.stack([jnp.sum(rows_f32, axis=1), jnp.sum(rows_f32 * rows_f32, axis=1)])
    row_sums = lax.psum(row_sums, "tp")
    row_mean = row_sums[0] / full_width
    row_var = row_sums[1] / full_width - row_mean * row_mean
    scaled = (rows_f32 - row_mean[:, None]) * lax.rsqrt(row_var + NORM_EPS)[:, None]
    return (scaled * norm_gain + norm_bias).astype(jnp.bfloat16)


def global_lse(logits):
    row_top = lax.pmax(jnp.max(logits, axis=1), ("vp", "tp"))
    exp_total = lax.psum(jnp.sum(jnp.exp(logits - row_top[:, None]), axis=1), ("vp", "tp"))
    return row_top + jnp.log(exp_total)


def solution(mesh):
    tp_size = mesh.shape["tp"]

    def per_device(hidden, lnf_gain, lnf_bias, emb_table, next_tok, eln_gain, eln_bias):
        full_width = hidden.shape[1] * tp_size
        normed = norm_shard(hidden, lnf_gain, lnf_bias, full_width)
        shard_logits = lax.dot_general(normed, emb_table, (((1,), (1,)), ((), ())), preferred_element_type=jnp.float32)
        logits = lax.psum_scatter(shard_logits, "tp", scatter_dimension=1, tiled=True)
        log_sum = global_lse(logits)
        logprobs = logits - log_sum[:, None]
        block_rows = emb_table.shape[0]
        local_idx = next_tok - lax.axis_index("vp") * block_rows
        is_owned = (local_idx >= 0) & (local_idx < block_rows)
        picked = jnp.take(emb_table, jnp.clip(local_idx, 0, block_rows - 1), axis=0).astype(jnp.float32)
        picked = jnp.where(is_owned[:, None], picked, jnp.zeros_like(picked))
        tok_rows = lax.psum(picked, "vp")
        next_in = norm_shard(tok_rows, eln_gain, eln_bias, full_width)
        return logprobs, log_sum, next_in

    return jax.shard_map(
        per_device,
        mesh=mesh,
        in_specs=(P("dp", "tp"), P("tp"), P("tp"), P("vp", "tp"), P("dp"), P("tp"), P("tp")),
        out_specs=(P("dp", ("vp", "tp")), P("dp"), P("dp", "tp")),
        check_vma=False,
    )
```

profile of v0, /device:TPU:0, one launch (start us, length us, event | category | flops | bytes accessed | tf_op | source)
XLA Modules:
  0.0 175.5 jit_solution(137122916970173947)
XLA Ops:
  7.2 0.0 reduce-scatter.2.cloned.1.call-start
  7.2 0.8 convert_reduce_fusion
  8.0 0.7 compare_and_fusion
  8.7 1.6 gather_fusion
  10.3 0.1 convert_select_fusion
  10.4 10.0 %psum.30 = f32[16,256]{1,0:T(8,128)S(1)} all-reduce(f32[16,256]{1,0:T(8,128)S(1)} %convert_select_fusion), channel_id=1, replica_groups=mesh['dp'=1,'vp'=2,'tp'=4] {'vp'}, use_global_device_ids=true, to_apply=%region_8.9 | all-reduce | flops 4096 | bytes 32768 | tf_op jit(solution)/shard_map/psum | solution.py:40
  20.4 0.1 fusion.15
  20.5 5.7 %all-reduce = (f32[2,16]{1,0:T(2,128)S(1)}, f32[2,16]{1,0:T(2,128)S(1)}) all-reduce(f32[2,16]{1,0:T(2,128)S(1)} %get-tuple-element.12, f32[2,16]{1,0:T(2,128)S(1)} %get-tuple-element.13), channel_id=1, replica_groups=mesh['dp'=1,'vp'=2,'tp'=4] {'tp'}, use_global_device_ids=true, to_apply=%region_2.0 | all-reduce | flops 64 | bytes 512 | tf_op jit(solution)/shard_map/psum | solution.py:12
  26.2 28.0 %fusion.5 = f32[16,125440]{1,0:T(8,128)} fusion(bf16[125440,256]{1,0:T(8,128)(2,1)} %param.10, bf16[16,256]{1,0:T(8,128)(2,1)} %param.7, f32[256]{0:T(256)} %param.9, f32[256]{0:T(256)} %param.8, f32[16]{0:T(128)S(1)} %fusion.14, f32[16]{0:T(128)S(1)} %multiply_bitcast_fusion.1), kind=kOutput, calls=%fused_computation.14 | convolution fusion | flops 1027629056 | bytes 72263808 | tf_op jit(solution)/shard_map/dot_general | solution.py:31
  54.1 0.0 reduce-scatter.2.cloned.1.call-update
  54.2 0.0 copy-start.1
  54.2 0.0 copy-start.2
  54.2 63.4 %reduce-scatter.2.cloned.1.call-done = f32[16,31360]{1,0:T(8,128)} async-done(((f32[16,125440]{1,0:T(8,128)}), f32[16,31360]{1,0:T(8,128)}) %reduce-scatter.2.cloned.1.call-update) | async-done | bytes 2007056 | tf_op jit(solution)/shard_map/reduce_scatter | solution.py:32
  117.6 0.0 copy-start
  117.6 2.1 %reduce_max.9 = f32[16]{0:T(128)S(1)} reduce(f32[16,31360]{1,0:T(8,128)} %reduce-scatter.2.cloned.1.call-done, f32[]{:T(128)} %constant.15.clone.1), dimensions={1}, to_apply=%region_4.0 | reduce | flops 501744 | bytes 2007108 | tf_op jit(solution)/shard_map/reduce_max | solution.py:20
  119.7 22.3 %pmax.7 = f32[16]{0:T(128)S(1)} all-reduce(f32[16]{0:T(128)S(1)} %reduce_max.9), channel_id=1, replica_groups=mesh['dp'=1,'vp'=2,'tp'=4] {'vp','tp'}, use_global_device_ids=true, to_apply=%region_5.0 | all-reduce | flops 16 | bytes 128 | tf_op jit(solution)/shard_map/pmax | solution.py:20
  141.9 0.0 copy-done
  142.0 0.6 exponential_reduce_fusion
  142.5 0.0 copy-done.1
  142.5 0.0 copy-done.2
  142.6 0.7 add_convert_fusion
  143.2 23.9 %psum.29 = f32[16]{0:T(128)S(1)} all-reduce(f32[16]{0:T(128)S(1)} %exponential_reduce_fusion), channel_id=1, replica_groups=mesh['dp'=1,'vp'=2,'tp'=4] {'vp','tp'}, use_global_device_ids=true, to_apply=%region_7.0 | all-reduce | flops 16 | bytes 128 | tf_op jit(solution)/shard_map/psum | solution.py:21
  167.2 0.0 copy-start.3
  167.2 1.5 broadcast_subtract_fusion
  168.6 0.0 copy-done.3
  (7 shorter events, 0.0 us)
Async XLA Ops:
  7.2 110.4 %reduce-scatter.2.cloned.1.call-start = ((), (), s32[]{:S(2)}) async-start(), calls=%async_computation.1 | async-start | bytes 10035200 | tf_op jit(solution)/shard_map/reduce_scatter | solution.py:32
  54.2 88.4 %copy-start.1 = (f32[256]{0:T(256)S(1)}, f32[256]{0:T(256)}, u32[]{:S(2)}) copy-start(f32[256]{0:T(256)} %param.13) | copy-start | bytes 3076
  54.2 88.3 %copy-start.2 = (f32[256]{0:T(256)S(1)}, f32[256]{0:T(256)}, u32[]{:S(2)}) copy-start(f32[256]{0:T(256)} %param.12) | copy-start | bytes 3076
  117.6 24.4 %copy-start = (f32[16,31360]{1,0:T(8,128)S(1)}, f32[16,31360]{1,0:T(8,128)}, u32[]{:S(2)}) copy-start(f32[16,31360]{1,0:T(8,128)} %reduce-scatter.2.cloned.1.call-done) | copy-start | bytes 6021124
  167.2 1.5 copy-start.3
Sparse Core Ops, SparseCore 0:
  54.3 63.2 reduce-scatter.1
where the time goes:
time: 176 us; the launch traced here: 175 us
  waiting for transfers between devices  63.4 us (36%)
  blocking collectives  61.8 us (35%)
  matrix products  28 us (16%)
  between operations  14.1 us (8%)
  other arithmetic  6.54 us (4%)
    reduce_scatter x1, waiting for transfers between devices, per_device(): lax.psum_scatter(shard_logits, 'tp', scatter_dimension=1, tiled=True)  63.4 us
    dot_general x1, matrix products, per_device(): lax.dot_general(normed, emb_table, (((1,), (1,)), ((), ())), preferred_el...  28 us
    psum x1, blocking collectives, global_lse(): lax.psum(jnp.sum(jnp.exp(logits - row_top[:, None]), axis=1), ('vp', 'tp'))  23.9 us
    pmax x1, blocking collectives, global_lse(): row_top = lax.pmax(jnp.max(logits, axis=1), ('vp', 'tp'))  22.3 us
    psum x1, blocking collectives, per_device(): tok_rows = lax.psum(picked, 'vp')  9.97 us
    psum x1, blocking collectives, norm_shard(): row_sums = lax.psum(row_sums, 'tp')  5.67 us
  transfers between devices with their start and end apart: 1, of which 1 were waited for; matrix products, arithmetic and copies ran while one was open for 0% of the time, Pallas kernels for 0%

commit v1 on v0

v1 whole, which is shorter than its diff:
```python
import functools

import jax
import jax.numpy as jnp
from jax import lax
from jax.experimental import pallas as pl
from jax.experimental.pallas import tpu as pltpu
from jax.sharding import PartitionSpec as P

NORM_EPS = 1e-5
MESH = pl.DeviceIdType.MESH
LANES = 128
SLOTS = 4
LAG = 3


def chunk_of(block):
    tiles = block // LANES
    return LANES * max(d for d in range(1, 9) if tiles % d == 0)


def pack_sums(rows_f32):
    sums = jnp.sum(rows_f32, axis=1, keepdims=True)
    squares = jnp.sum(rows_f32 * rows_f32, axis=1, keepdims=True)
    shape = (rows_f32.shape[0], LANES)
    lane = lax.broadcasted_iota(jnp.int32, shape, 1)
    return jnp.where(lane < LANES // 2, jnp.broadcast_to(sums, shape), jnp.broadcast_to(squares, shape))


def apply_norm(rows_f32, packed, gain, bias, full_width):
    half = LANES // 2
    mean = packed[:, 0:1] / full_width
    var = packed[:, half : half + 1] / full_width - mean * mean
    scaled = (rows_f32 - mean) * lax.rsqrt(var + NORM_EPS)
    return (scaled * gain + bias).astype(jnp.bfloat16)


def main_kernel(
    vp_size, chunk, n_chunks, full_width,
    hid_ref, g1_ref, b1_ref, table_ref, pick_ref, g2_ref, b2_ref,
    z_ref, ls_ref, nxt_ref,
    tab, xn, mine, give, take, land, st, row_in, es, fs,
    tab_sem, give_sem, take_sem, push_sem, land_sem,
    st_ssem, st_rsem, row_ssem, row_rsem, es_ssem, es_rsem, fs_ssem, fs_rsem,
):
    v = lax.axis_index("vp")
    t = lax.axis_index("tp")
    n_dev = vp_size * 4
    me = v * 4 + t
    core = t % 2
    chip = t // 2
    sib = chip * 2 + 1 - core
    across = (1 - chip) * 2 + core
    diag = (1 - chip) * 2 + 1 - core
    block = chunk * n_chunks
    n_steps = 2 * n_chunks

    def table_copy(step, part):
        far = 1 - step // n_chunks
        owner_chip = chip + far - 2 * chip * far
        owner_core = core + (1 - part) - 2 * core * (1 - part)
        start = (owner_chip * 2 + owner_core) * block + (step % n_chunks) * chunk
        slot = step % SLOTS
        return pltpu.make_async_copy(
            table_ref.at[pl.ds(pl.multiple_of(start, LANES), chunk), :],
            tab.at[slot, part],
            tab_sem.at[slot, part],
        )

    for s in range(SLOTS):
        table_copy(s, 0).start()
        table_copy(s, 1).start()

    barrier = pltpu.get_barrier_semaphore()
    for d in range(1, n_dev):
        other = (me + d) % n_dev
        pl.semaphore_signal(barrier, inc=1, device_id={"vp": other // 4, "tp": other % 4}, device_id_type=MESH)

    hid = hid_ref[...].astype(jnp.float32)
    st[t] = pack_sums(hid)
    pl.semaphore_wait(barrier, n_dev - 1)

    stat_copies = []
    for i, target in enumerate((across, diag, sib)):
        copy = pltpu.make_async_remote_copy(
            st.at[t], st.at[t], st_ssem.at[i], st_rsem.at[i], device_id={"tp": target}, device_id_type=MESH
        )
        copy.start()
        stat_copies.append(copy)
    row_copies = []
    for d in range(1, vp_size):
        copy = pltpu.make_async_remote_copy(
            pick_ref, row_in.at[d - 1], row_ssem.at[d - 1], row_rsem.at[d - 1],
            device_id={"vp": (v + d) % vp_size}, device_id_type=MESH,
        )
        copy.start()
        row_copies.append(copy)
    for copy in stat_copies:
        copy.wait_recv()
    total = st[0] + st[1] + st[2] + st[3]
    xn[...] = apply_norm(hid, total, g1_ref[...], b1_ref[...], full_width)

    def give_copy(step):
        return pltpu.make_async_remote_copy(
            give.at[step], take.at[step], give_sem.at[step], take_sem.at[step],
            device_id={"tp": sib}, device_id_type=MESH,
        )

    def push_copy(j):
        return pltpu.make_async_remote_copy(
            mine.at[j], land.at[j], push_sem.at[j], land_sem.at[j],
            device_id={"tp": across}, device_id_type=MESH,
        )

    def dot_part(slot, part):
        return lax.dot_general(
            xn[...], tab[slot, part], (((1,), (1,)), ((), ())), preferred_element_type=jnp.float32
        )

    def combine(step):
        give_copy(step).wait_recv()
        mine[step] = mine[step] + take[step]

    def produce(step):
        slot = step % SLOTS
        table_copy(step, 0).wait()
        give[step] = dot_part(slot, 0)
        give_copy(step).start()
        table_copy(step, 1).wait()
        mine[step] = dot_part(slot, 1)

        @pl.when(step + SLOTS < n_steps)
        def _():
            table_copy(step + SLOTS, 0).start()
            table_copy(step + SLOTS, 1).start()

    def far_step(step, carry):
        produce(step)

        @pl.when(step >= LAG)
        def _():
            combine(step - LAG)
            push_copy(step - LAG).start()

        return carry

    lax.fori_loop(0, n_chunks, far_step, 0)
    for j in range(n_chunks - LAG, n_chunks):
        combine(j)
        push_copy(j).start()

    rows = pick_ref[...]
    for d in range(1, vp_size):
        row_copies[d - 1].wait_recv()
        rows = rows + row_in[d - 1]
    es[t] = pack_sums(rows)
    sum_copies = []
    for i, target in enumerate((across, diag, sib)):
        copy = pltpu.make_async_remote_copy(
            es.at[t], es.at[t], es_ssem.at[i], es_rsem.at[i], device_id={"tp": target}, device_id_type=MESH
        )
        copy.start()
        sum_copies.append(copy)

    def near_step(step, carry):
        produce(step)

        @pl.when(step >= n_chunks + LAG)
        def _():
            combine(step - LAG)

        return carry

    lax.fori_loop(n_chunks, n_steps, near_step, 0)
    for j in range(n_steps - LAG, n_steps):
        combine(j)

    for copy in sum_copies:
        copy.wait_recv()
    row_total = es[0] + es[1] + es[2] + es[3]
    nxt_ref[...] = apply_norm(rows, row_total, g2_ref[...], b2_ref[...], full_width)

    n_rows = hid.shape[0]

    def finish(j, carry):
        top, acc = carry
        push_copy(j).wait_recv()
        vals = mine[n_chunks + j] + land[j]
        z_ref[:, pl.ds(pl.multiple_of(j * chunk, LANES), chunk)] = vals
        tiles = [vals[:, i * LANES : (i + 1) * LANES] for i in range(chunk // LANES)]
        new_top = functools.reduce(jnp.maximum, tiles, top)
        acc = acc * jnp.exp(top - new_top)
        for tile in tiles:
            acc = acc + jnp.exp(tile - new_top)
        return new_top, acc

    top, acc = lax.fori_loop(
        0, n_chunks, finish,
        (jnp.full((n_rows, LANES), -jnp.inf, jnp.float32), jnp.zeros((n_rows, LANES), jnp.float32)),
    )
    row_top = jnp.max(top, axis=1, keepdims=True)
    row_sum = jnp.sum(acc * jnp.exp(top - row_top), axis=1, keepdims=True)
    lane = lax.broadcasted_iota(jnp.int32, (n_rows, LANES), 1)
    fs[me] = jnp.where(
        lane < LANES // 2, jnp.broadcast_to(row_top, (n_rows, LANES)), jnp.broadcast_to(row_sum, (n_rows, LANES))
    )
    last_copies = []
    for d in range(1, n_dev):
        other = (me + d) % n_dev
        copy = pltpu.make_async_remote_copy(
            fs.at[me], fs.at[me], fs_ssem.at[d - 1], fs_rsem.at[d - 1],
            device_id={"vp": other // 4, "tp": other % 4}, device_id_type=MESH,
        )
        copy.start()
        last_copies.append(copy)
    for copy in last_copies:
        copy.wait_recv()
    half = LANES // 2
    all_top = functools.reduce(jnp.maximum, [fs[i][:, 0:half] for i in range(n_dev)])
    all_sum = jnp.zeros_like(all_top)
    for i in range(n_dev):
        all_sum = all_sum + fs[i][:, half:] * jnp.exp(fs[i][:, 0:half] - all_top)
    ls_ref[...] = all_top + jnp.log(all_sum)

    for copy in stat_copies + row_copies + sum_copies + last_copies:
        copy.wait_send()

    def drain(step, carry):
        give_copy(step).wait_send()
        return carry

    lax.fori_loop(0, n_steps, drain, 0)

    def drain_push(j, carry):
        push_copy(j).wait_send()
        return carry

    lax.fori_loop(0, n_chunks, drain_push, 0)


def solution(mesh):
    tp_size = mesh.shape["tp"]
    vp_size = mesh.shape["vp"]

    def per_device(hidden, lnf_gain, lnf_bias, emb_table, next_tok, eln_gain, eln_bias):
        n_rows, width = hidden.shape
        full_width = width * tp_size
        block_rows = emb_table.shape[0]
        block = block_rows // tp_size
        chunk = chunk_of(block)
        n_chunks = block // chunk
        n_dev = tp_size * vp_size

        local_idx = next_tok - lax.axis_index("vp") * block_rows
        is_owned = (local_idx >= 0) & (local_idx < block_rows)
        picked = jnp.take(emb_table, jnp.clip(local_idx, 0, block_rows - 1), axis=0).astype(jnp.float32)
        picked = jnp.where(is_owned[:, None], picked, jnp.zeros_like(picked))

        dma = pltpu.SemaphoreType.DMA
        vmem = pl.BlockSpec(memory_space=pltpu.VMEM)
        z, ls, next_in = pl.pallas_call(
            functools.partial(main_kernel, vp_size, chunk, n_chunks, full_width),
            out_shape=(
                jax.ShapeDtypeStruct((n_rows, block), jnp.float32),
                jax.ShapeDtypeStruct((n_rows, LANES // 2), jnp.float32),
                jax.ShapeDtypeStruct((n_rows, width), jnp.bfloat16),
            ),
            in_specs=[vmem, vmem, vmem, pl.BlockSpec(memory_space=pl.ANY), vmem, vmem, vmem],
            out_specs=(vmem, vmem, vmem),
            scratch_shapes=[
                pltpu.VMEM((SLOTS, 2, chunk, width), jnp.bfloat16),
                pltpu.VMEM((n_rows, width), jnp.bfloat16),
                pltpu.VMEM((2 * n_chunks, n_rows, chunk), jnp.float32),
                pltpu.VMEM((2 * n_chunks, n_rows, chunk), jnp.float32),
                pltpu.VMEM((2 * n_chunks, n_rows, chunk), jnp.float32),
                pltpu.VMEM((n_chunks, n_rows, chunk), jnp.float32),
                pltpu.VMEM((tp_size, n_rows, LANES), jnp.float32),
                pltpu.VMEM((max(vp_size - 1, 1), n_rows, width), jnp.float32),
                pltpu.VMEM((tp_size, n_rows, LANES), jnp.float32),
                pltpu.VMEM((n_dev, n_rows, LANES), jnp.float32),
                dma((SLOTS, 2)),
                dma((2 * n_chunks,)),
                dma((2 * n_chunks,)),
                dma((n_chunks,)),
                dma((n_chunks,)),
                dma((tp_size - 1,)),
                dma((tp_size - 1,)),
                dma((max(vp_size - 1, 1),)),
                dma((max(vp_size - 1, 1),)),
                dma((tp_size - 1,)),
                dma((tp_size - 1,)),
                dma((n_dev - 1,)),
                dma((n_dev - 1,)),
            ],
            compiler_params=pltpu.CompilerParams(collective_id=0, has_side_effects=True),
        )(
            hidden, lnf_gain.reshape(1, width), lnf_bias.reshape(1, width), emb_table, picked,
            eln_gain.reshape(1, width), eln_bias.reshape(1, width),
        )
        log_sum = ls[:, 0]
        logprobs = z - log_sum[:, None]
        return logprobs, log_sum, next_in

    return jax.shard_map(
        per_device,
        mesh=mesh,
        in_specs=(P("dp", "tp"), P("tp"), P("tp"), P("vp", "tp"), P("dp"), P("tp"), P("tp")),
        out_specs=(P("dp", ("vp", "tp")), P("dp"), P("dp", "tp")),
        check_vma=False,
    )
```

time: 176 us -> 71.7 us (0.41)
  waiting for transfers between devices: 63.4 us -> 0 us
  Pallas kernels: 0 us -> 63.3 us
  blocking collectives: 61.8 us -> 0 us
  matrix products: 28 us -> 0 us
  between operations: 14.1 us -> 0.66 us
  other arithmetic: 6.54 us -> 4.4 us
    reduce_scatter x1 -> x0, waiting for transfers between devices: 63.4 us -> none  [per_device(): lax.psum_scatter(shard_logits, 'tp', scatter_dimension=1, tiled=True)]
    pallas_call x0 -> x1, Pallas kernels: none -> 63.3 us  [per_device(): pl.pallas_call(functools.partial(main_kernel, vp_size, chunk, n_chunks, f...]
    psum x3 -> x0, blocking collectives: 39.6 us -> none  [the longest x1 23.9 us: global_lse(): lax.psum(jnp.sum(jnp.exp(logits - row_top[:, None]), axis=1), ('vp', 'tp'))]
    dot_general x1 -> x0, matrix products: 28 us -> none  [per_device(): lax.dot_general(normed, emb_table, (((1,), (1,)), ((), ())), preferred_el...]
    pmax x1 -> x0, blocking collectives: 22.3 us -> none  [global_lse(): row_top = lax.pmax(jnp.max(logits, axis=1), ('vp', 'tp'))]
    reduce_max x1 -> x0, other arithmetic: 2.07 us -> none  [global_lse(): row_top = lax.pmax(jnp.max(logits, axis=1), ('vp', 'tp'))]
  transfers between devices with their start and end apart: 1 -> 0, of which waited for: 1 -> 0; matrix products, arithmetic and copies ran while one was open for 0% -> 0% of each run, Pallas kernels for 0% -> 0%
where the time goes in v1:
time: 71.7 us; the launch traced here: 71.4 us
  Pallas kernels  63.3 us (88%)
  other arithmetic  4.4 us (6%)
  local copies, waits for them, and re-layouts  3.04 us (4%)
    pallas_call x1, Pallas kernels, per_device(): pl.pallas_call(functools.partial(main_kernel, vp_size, chunk, n_chunks, f...  63.3 us
    sub x1, other arithmetic, per_device(): logprobs = z - log_sum[:, None]  3.05 us
    gather x1, local copies, waits for them, and re-layouts, per_device(): jnp.take(emb_table, jnp.clip(local_idx, 0, block_rows - 1), axis=0)  1.62 us

profile of v1, /device:TPU:0, one launch (start us, length us, event | category | flops | bytes accessed | tf_op | source)
XLA Modules:
  0.0 71.4 jit_solution(10916996078351555670)
XLA Ops:
  0.6 0.7 compare_and_fusion
  1.3 1.6 %gather_fusion = bf16[16,256]{1,0:T(8,128)(2,1)S(1)} fusion(bf16[125440,256]{1,0:T(8,128)(2,1)} %table_ref.1, s32[1024]{0:T(1024)S(1)} %pad_clamp_fusion), kind=kCustom, calls=%fused_computation | custom fusion | bytes 16448 | tf_op jit(solution)/shard_map/jit(_take)/gather | solution.py:256
  2.9 0.7 convert_select_fusion.pick_ref
  3.6 63.3 %shard_map.94 = (f32[16,31360]{1,0:T(8,128)}, f32[16,64]{1,0:T(8,128)}, bf16[16,256]{1,0:T(8,128)(2,1)}) custom-call(bf16[16,256]{1,0:T(8,128)(2,1)} %hid_ref.1, f32[1,256]{1,0:T(1,128)} %bitcast.4, f32[1,256]{1,0:T(1,128)} %bitcast.5, bf16[125440,256]{1,0:T(8,128)(2,1)} %table_ref.1, f32[16,256]{1,0:T(8,128)} %convert_select_fusion.pick_ref, ...), custom_call_target="tpu_custom_call" | custom-call | tf_op jit(solution)/shard_map/pallas_call | solution.py:261
  66.9 0.8 %slice_reduce_fusion = f32[16]{0:T(128)S(1)} fusion(f32[16,64]{1,0:T(8,128)} %get-tuple-element.7), kind=kLoop, calls=%fused_computation.3 | loop fusion | bytes 128 | tf_op jit(solution)/shard_map/slice | solution.py:300
  67.7 0.0 copy-start.1
  67.7 0.0 copy-start
  67.7 3.0 %broadcast_subtract_fusion = f32[16,31360]{1,0:T(8,128)} fusion(f32[16,31360]{1,0:T(8,128)} %get-tuple-element.6, f32[16]{0:T(128)S(1)} %slice_reduce_fusion), kind=kLoop, calls=%fused_computation.1 | loop fusion | flops 501760 | bytes 4014144 | tf_op jit(solution)/shard_map/sub | solution.py:301
  70.8 0.0 copy-done.1
  70.8 0.0 copy-done
  70.8 0.6 copy.11
  (1 shorter events, 0.0 us)
Async XLA Ops:
  67.7 3.1 %copy-start.1 = (f32[16]{0:T(128)}, f32[16]{0:T(128)S(1)}, u32[]{:S(2)}) copy-start(f32[16]{0:T(128)S(1)} %slice_reduce_fusion) | copy-start | bytes 196
  67.7 3.1 %copy-start = (bf16[16,256]{1,0:T(8,128)(2,1)S(1)}, bf16[16,256]{1,0:T(8,128)(2,1)}, u32[]{:S(2)}) copy-start(bf16[16,256]{1,0:T(8,128)(2,1)} %get-tuple-element.17) | copy-start | bytes 24580

commit v2 on v0

v2 whole, which is shorter than its diff:
```python
import functools

import jax
import jax.numpy as jnp
from jax import lax
from jax.experimental import pallas as pl
from jax.experimental.pallas import tpu as pltpu
from jax.sharding import PartitionSpec as P

NORM_EPS = 1e-5
MESH = pl.DeviceIdType.MESH
LANES = 128
CHUNK = 1792
SLOTS = 4
OUT_PARTS = 7


def row_sums(rows_f32):
    return jnp.sum(rows_f32, axis=1, keepdims=True), jnp.sum(rows_f32 * rows_f32, axis=1, keepdims=True)


def pack_lanes(columns):
    shape = (columns[0].shape[0], LANES)
    lane = lax.broadcasted_iota(jnp.int32, shape, 1)
    span = LANES // len(columns)
    packed = jnp.broadcast_to(columns[0], shape)
    for i, column in enumerate(columns[1:], 1):
        packed = jnp.where(lane >= i * span, jnp.broadcast_to(column, shape), packed)
    return packed


def apply_norm(rows_f32, sums, squares, gain, bias, full_width):
    mean = sums / full_width
    var = squares / full_width - mean * mean
    scaled = (rows_f32 - mean) * lax.rsqrt(var + NORM_EPS)
    return (scaled * gain + bias).astype(jnp.bfloat16)


def main_kernel(
    vp_size, first, n_chunks, full_width,
    hid_hbm, g1_hbm, b1_hbm, table_ref, tok_hbm, g2_hbm, b2_hbm,
    z_ref, sums_ref, rows_ref, affine_ref,
    hid_ref, g1_ref, b1_ref, tok_ref, tab, xn, mine, give, take, land, mine0, give0, take0, land0,
    st, row_own, row_in, fs,
    in_sem, tab_sem, give_sem, take_sem, push_sem, land_sem, st_ssem, st_rsem, row_ssem, row_rsem, fs_ssem, fs_rsem,
):
    v = lax.axis_index("vp")
    t = lax.axis_index("tp")
    n_dev = vp_size * 4
    me = v * 4 + t
    core = t % 2
    chip = t // 2
    sib = chip * 2 + 1 - core
    across = (1 - chip) * 2 + core
    diag = (1 - chip) * 2 + 1 - core
    block = first + CHUNK * n_chunks

    barrier = pltpu.get_barrier_semaphore()
    for d in range(1, n_dev):
        other = (me + d) % n_dev
        pl.semaphore_signal(barrier, inc=1, device_id={"vp": other // 4, "tp": other % 4}, device_id_type=MESH)

    small = [
        pltpu.make_async_copy(src, dst, in_sem.at[i])
        for i, (src, dst) in enumerate((
            (hid_hbm, hid_ref), (g1_hbm, g1_ref), (b1_hbm, b1_ref), (tok_hbm, tok_ref),
            (g2_hbm, affine_ref.at[pl.ds(0, 1)]), (b2_hbm, affine_ref.at[pl.ds(1, 1)]),
        ))
    ]
    for copy in small:
        copy.start()

    def table_start(phase, step, part):
        owner_chip = (1 - chip) if phase == 0 else chip
        owner_core = (1 - core) if part == 0 else core
        base = (owner_chip * 2 + owner_core) * block
        return base if isinstance(step, int) and step == 0 else base + first + (step - 1) * CHUNK

    def table_copy(phase, step, slot, part):
        size = first if isinstance(step, int) and step == 0 else CHUNK
        start = pl.multiple_of(table_start(phase, step, part), LANES)
        return pltpu.make_async_copy(
            table_ref.at[pl.ds(start, size), :], tab.at[slot, part, pl.ds(0, size)], tab_sem.at[slot, part]
        )

    per_phase = n_chunks + 1

    def prefetch(phase, step):
        slot = (phase * per_phase + step) % SLOTS
        for part in range(2):
            table_copy(phase, step, slot, part).start()

    for s in range(SLOTS):
        prefetch(0, s)

    small[0].wait()
    hid = hid_ref[...].astype(jnp.float32)
    st[t] = pack_lanes(row_sums(hid))
    pl.semaphore_wait(barrier, n_dev - 1)

    stat_copies = []
    for i, target in enumerate((across, diag, sib)):
        copy = pltpu.make_async_remote_copy(
            st.at[t], st.at[t], st_ssem.at[i], st_rsem.at[i], device_id={"tp": target}, device_id_type=MESH
        )
        copy.start()
        stat_copies.append(copy)

    for copy in small[1:]:
        copy.wait()
    n_rows = hid.shape[0]
    on_diag = lax.broadcasted_iota(jnp.int32, (n_rows, n_rows), 0) == lax.broadcasted_iota(jnp.int32, (n_rows, n_rows), 1)
    tok_f32 = jnp.broadcast_to(tok_ref[...].astype(jnp.float32), (n_rows, n_rows))
    tok_col = jnp.sum(jnp.where(on_diag, tok_f32, 0.0), axis=1, keepdims=True).astype(jnp.int32)
    tok_col = tok_col - v * (4 * block)
    row_own[...] = jnp.zeros_like(row_own)

    for copy in stat_copies:
        copy.wait_recv()
    total = st[0] + st[1] + st[2] + st[3]
    half = LANES // 2
    xn[...] = apply_norm(hid, total[:, 0:1], total[:, half : half + 1], g1_ref[...], b1_ref[...], full_width)

    def bufs(phase, step):
        if isinstance(step, int) and step == 0:
            return mine0.at[phase], give0.at[phase], take0.at[phase], land0, phase * per_phase
        i = phase * n_chunks + step - 1
        return mine.at[i], give.at[i], take.at[i], land.at[step - 1], phase * per_phase + step

    def give_copy(phase, step):
        _, src, dst, _, k = bufs(phase, step)
        return pltpu.make_async_remote_copy(
            src, dst, give_sem.at[k], take_sem.at[k], device_id={"tp": sib}, device_id_type=MESH
        )

    def push_copy(step):
        src, _, _, dst, k = bufs(0, step)
        return pltpu.make_async_remote_copy(
            src, dst, push_sem.at[k], land_sem.at[k], device_id={"tp": across}, device_id_type=MESH
        )

    def combine(phase, step):
        own, _, got, _, _ = bufs(phase, step)
        give_copy(phase, step).wait_recv()
        own[...] = own[...] + got[...]
        if phase == 0:
            push_copy(step).start()

    def produce(phase, step, select=True):
        size = first if isinstance(step, int) and step == 0 else CHUNK
        slot = (phase * per_phase + step) % SLOTS
        own, out, _, _, _ = bufs(phase, step)
        for part, dst in enumerate((out, own)):
            table_copy(phase, step, slot, part).wait()
            dst[...] = lax.dot_general(
                xn[...], tab[slot, part, 0:size, :], (((1,), (1,)), ((), ())), preferred_element_type=jnp.float32
            )
            if select:
                select_part(phase, step, part)
            if part == 0:
                give_copy(phase, step).start()

    def select_part(phase, step, part):
        size = first if isinstance(step, int) and step == 0 else CHUNK
        slot = (phase * per_phase + step) % SLOTS
        at = tok_col - table_start(phase, step, part)
        hit = lax.broadcasted_iota(jnp.int32, (n_rows, size), 1) == at
        ones = jnp.where(hit, 1.0, 0.0).astype(jnp.bfloat16)
        row_own[...] = row_own[...] + jnp.dot(ones, tab[slot, part, 0:size, :], preferred_element_type=jnp.float32)

    produce(0, 0, select=False)
    produce(0, 1, select=False)
    combine(0, 0)
    for step in range(2):
        for part in range(2):
            select_part(0, step, part)
        prefetch(0, SLOTS + step)

    def far_step(step, carry, next_phase=0):
        produce(0, step)
        combine(0, step - 1)
        prefetch(next_phase, step + SLOTS - next_phase * per_phase)
        return carry

    lax.fori_loop(2, per_phase - SLOTS, far_step, 0)
    produce(0, per_phase - SLOTS)
    combine(0, per_phase - SLOTS - 1)
    prefetch(1, 0)
    lax.fori_loop(per_phase - SLOTS + 1, per_phase, functools.partial(far_step, next_phase=1), 0)

    produce(1, 0)
    combine(0, n_chunks)
    prefetch(1, SLOTS)
    produce(1, 1)
    combine(1, 0)
    prefetch(1, SLOTS + 1)

    def near_step(step, carry):
        produce(1, step)
        combine(1, step - 1)

        @pl.when(step + SLOTS < per_phase)
        def _():
            prefetch(1, step + SLOTS)

        return carry

    lax.fori_loop(2, per_phase, near_step, 0)

    row_copies = []
    for d in range(1, vp_size):
        copy = pltpu.make_async_remote_copy(
            row_own, row_in.at[d - 1], row_ssem.at[d - 1], row_rsem.at[d - 1],
            device_id={"vp": (v + d) % vp_size}, device_id_type=MESH,
        )
        copy.start()
        row_copies.append(copy)
    combine(1, n_chunks)
    own_sums, own_squares = row_sums(row_own[...])

    def finish(step, carry):
        size, offset = (first, 0) if isinstance(step, int) and step == 0 else (CHUNK, first + (step - 1) * CHUNK)
        top, acc = carry
        own, _, _, _, _ = bufs(1, step)
        _, _, _, got, _ = bufs(0, step)
        push_copy(step).wait_recv()
        vals = own[...] + got[...]
        z_ref[:, pl.ds(pl.multiple_of(offset, LANES), size)] = vals
        tiles = [vals[:, i * LANES : (i + 1) * LANES] for i in range(size // LANES)]
        new_top = functools.reduce(jnp.maximum, tiles, top)
        acc = acc * jnp.exp(top - new_top)
        for tile in tiles:
            acc = acc + jnp.exp(tile - new_top)
        return new_top, acc

    state = (jnp.full((n_rows, LANES), -jnp.inf, jnp.float32), jnp.zeros((n_rows, LANES), jnp.float32))
    state = finish(0, state)
    top, acc = lax.fori_loop(1, per_phase, finish, state)
    row_top = jnp.max(top, axis=1, keepdims=True)
    row_sum = jnp.sum(acc * jnp.exp(top - row_top), axis=1, keepdims=True)
    fs[me] = pack_lanes((row_top, row_sum, own_sums, own_squares))
    last_copies = []
    for d in range(1, n_dev):
        other = (me + d) % n_dev
        copy = pltpu.make_async_remote_copy(
            fs.at[me], fs.at[me], fs_ssem.at[d - 1], fs_rsem.at[d - 1],
            device_id={"vp": other // 4, "tp": other % 4}, device_id_type=MESH,
        )
        copy.start()
        last_copies.append(copy)

    rows = row_own[...]
    for d in range(1, vp_size):
        row_copies[d - 1].wait_recv()
        rows = rows + row_in[d - 1]
    rows_ref[...] = rows
    for copy in stat_copies + row_copies:
        copy.wait_send()
    for phase in range(2):
        give_copy(phase, 0).wait_send()

        def drain(step, carry, phase=phase):
            give_copy(phase, step).wait_send()
            if phase == 0:
                push_copy(step).wait_send()
            return carry

        lax.fori_loop(1, per_phase, drain, 0)
    push_copy(0).wait_send()

    for copy in last_copies:
        copy.wait()
    sums_ref[...] = fs[...]


def tail_kernel(
    n_dev, full_width, z_ref, sums_ref, rows_ref, affine_ref, out_hbm, ls_hbm, nxt_hbm, out, ls, nxt, sem
):
    quarter = LANES // 4
    packed = [sums_ref[i] for i in range(n_dev)]
    all_top = functools.reduce(jnp.maximum, [p[:, 0:1] for p in packed])
    all_sum = functools.reduce(jnp.add, [p[:, quarter : quarter + 1] * jnp.exp(p[:, 0:1] - all_top) for p in packed])
    log_sum = all_top + jnp.log(all_sum)
    n_rows, block = out.shape
    part = block // OUT_PARTS
    copies = []
    for i in range(OUT_PARTS):
        columns = pl.ds(i * part, part)
        out[:, columns] = z_ref[:, columns] - log_sum
        copy = pltpu.make_async_copy(out.at[:, columns], out_hbm.at[:, columns], sem.at[i])
        copy.start()
        copies.append(copy)
    on_diag = lax.broadcasted_iota(jnp.int32, (n_rows, n_rows), 0) == lax.broadcasted_iota(jnp.int32, (n_rows, n_rows), 1)
    ls[...] = jnp.sum(jnp.where(on_diag, jnp.broadcast_to(log_sum, (n_rows, n_rows)), 0.0), axis=0, keepdims=True)
    copy = pltpu.make_async_copy(ls, ls_hbm, sem.at[OUT_PARTS])
    copy.start()
    copies.append(copy)
    sums = functools.reduce(jnp.add, [p[:, 2 * quarter : 2 * quarter + 1] for p in packed])
    squares = functools.reduce(jnp.add, [p[:, 3 * quarter : 3 * quarter + 1] for p in packed])
    nxt[...] = apply_norm(rows_ref[...], sums, squares, affine_ref[0:1, :], affine_ref[1:2, :], full_width)
    copy = pltpu.make_async_copy(nxt, nxt_hbm, sem.at[OUT_PARTS + 1])
    copy.start()
    copies.append(copy)
    for copy in copies:
        copy.wait()


def solution(mesh):
    tp_size = mesh.shape["tp"]
    vp_size = mesh.shape["vp"]
    n_dev = tp_size * vp_size

    def per_device(hidden, lnf_gain, lnf_bias, emb_table, next_tok, eln_gain, eln_bias):
        n_rows, width = hidden.shape
        full_width = width * tp_size
        block = emb_table.shape[0] // tp_size
        n_chunks = block // CHUNK
        first = block - n_chunks * CHUNK
        per_phase = n_chunks + 1

        dma = pltpu.SemaphoreType.DMA
        f32 = jnp.float32
        hbm = pl.BlockSpec(memory_space=pl.ANY)
        vmem = pl.BlockSpec(memory_space=pltpu.VMEM)
        row = lambda a: a.reshape(1, a.shape[0])
        z, sums, rows, affine = pl.pallas_call(
            functools.partial(main_kernel, vp_size, first, n_chunks, full_width),
            out_shape=(
                pltpu.VMEM((n_rows, block), f32),
                pltpu.VMEM((n_dev, n_rows, LANES), f32),
                pltpu.VMEM((n_rows, width), f32),
                pltpu.VMEM((2, width), f32),
            ),
            in_specs=[pl.BlockSpec(memory_space=pltpu.HBM)] * 7,
            out_specs=(vmem,) * 4,
            scratch_shapes=[
                pltpu.VMEM((n_rows, width), jnp.bfloat16),
                pltpu.VMEM((1, width), f32),
                pltpu.VMEM((1, width), f32),
                pltpu.VMEM((1, n_rows), jnp.int32),
                pltpu.VMEM((SLOTS, 2, CHUNK, width), jnp.bfloat16),
                pltpu.VMEM((n_rows, width), jnp.bfloat16),
                pltpu.VMEM((2 * n_chunks, n_rows, CHUNK), f32),
                pltpu.VMEM((2 * n_chunks, n_rows, CHUNK), f32),
                pltpu.VMEM((2 * n_chunks, n_rows, CHUNK), f32),
                pltpu.VMEM((n_chunks, n_rows, CHUNK), f32),
                pltpu.VMEM((2, n_rows, first), f32),
                pltpu.VMEM((2, n_rows, first), f32),
                pltpu.VMEM((2, n_rows, first), f32),
                pltpu.VMEM((n_rows, first), f32),
                pltpu.VMEM((tp_size, n_rows, LANES), f32),
                pltpu.VMEM((n_rows, width), f32),
                pltpu.VMEM((vp_size - 1, n_rows, width), f32),
                pltpu.VMEM((n_dev, n_rows, LANES), f32),
                dma((6,)),
                dma((SLOTS, 2)),
                dma((2 * per_phase,)),
                dma((2 * per_phase,)),
                dma((per_phase,)),
                dma((per_phase,)),
                dma((tp_size - 1,)),
                dma((tp_size - 1,)),
                dma((vp_size - 1,)),
                dma((vp_size - 1,)),
                dma((n_dev - 1,)),
                dma((n_dev - 1,)),
            ],
            compiler_params=pltpu.CompilerParams(
                collective_id=0, has_side_effects=True, vmem_limit_bytes=40 * 2**20
            ),
        )(*(
            pltpu.with_memory_space_constraint(a, pltpu.HBM)
            for a in (hidden, row(lnf_gain), row(lnf_bias), emb_table, row(next_tok), row(eln_gain), row(eln_bias))
        ))
        logprobs, log_sum, next_in = pl.pallas_call(
            functools.partial(tail_kernel, n_dev, full_width),
            out_shape=(
                jax.ShapeDtypeStruct((n_rows, block), f32),
                jax.ShapeDtypeStruct((1, n_rows), f32),
                jax.ShapeDtypeStruct((n_rows, width), jnp.bfloat16),
            ),
            in_specs=[vmem] * 4,
            out_specs=(hbm,) * 3,
            scratch_shapes=[
                pltpu.VMEM((n_rows, block), f32),
                pltpu.VMEM((1, n_rows), f32),
                pltpu.VMEM((n_rows, width), jnp.bfloat16),
                dma((OUT_PARTS + 2,)),
            ],
            compiler_params=pltpu.CompilerParams(vmem_limit_bytes=12 * 2**20),
        )(*(pltpu.with_memory_space_constraint(a, pltpu.VMEM) for a in (z, sums, rows, affine)))
        return logprobs, log_sum.reshape(n_rows), next_in

    return jax.shard_map(
        per_device,
        mesh=mesh,
        in_specs=(P("dp", "tp"), P("tp"), P("tp"), P("vp", "tp"), P("dp"), P("tp"), P("tp")),
        out_specs=(P("dp", ("vp", "tp")), P("dp"), P("dp", "tp")),
        check_vma=False,
    )
```

time: 176 us -> 60.9 us (0.35)
  waiting for transfers between devices: 63.4 us -> 0 us
  blocking collectives: 61.8 us -> 0 us
  Pallas kernels: 0 us -> 60.1 us
  matrix products: 28 us -> 0 us
  between operations: 14.1 us -> 0.64 us
  other arithmetic: 6.54 us -> 0 us
    reduce_scatter x1 -> x0, waiting for transfers between devices: 63.4 us -> none  [per_device(): lax.psum_scatter(shard_logits, 'tp', scatter_dimension=1, tiled=True)]
    pallas_call x0 -> x2, Pallas kernels: none -> 60.1 us  [the longest x1 58.5 us: per_device(): pl.pallas_call(functools.partial(main_kernel, vp_size, first, n_chunks, f...]
    psum x3 -> x0, blocking collectives: 39.6 us -> none  [the longest x1 23.9 us: global_lse(): lax.psum(jnp.sum(jnp.exp(logits - row_top[:, None]), axis=1), ('vp', 'tp'))]
    dot_general x1 -> x0, matrix products: 28 us -> none  [per_device(): lax.dot_general(normed, emb_table, (((1,), (1,)), ((), ())), preferred_el...]
    pmax x1 -> x0, blocking collectives: 22.3 us -> none  [global_lse(): row_top = lax.pmax(jnp.max(logits, axis=1), ('vp', 'tp'))]
    reduce_max x1 -> x0, other arithmetic: 2.07 us -> none  [global_lse(): row_top = lax.pmax(jnp.max(logits, axis=1), ('vp', 'tp'))]
  transfers between devices with their start and end apart: 1 -> 0, of which waited for: 1 -> 0; matrix products, arithmetic and copies ran while one was open for 0% -> 0% of each run, Pallas kernels for 0% -> 0%
where the time goes in v2:
time: 60.9 us; the launch traced here: 60.8 us
  Pallas kernels  60.1 us (99%)
  between operations  0.64 us (1%)
    pallas_call x1, Pallas kernels, per_device(): pl.pallas_call(functools.partial(main_kernel, vp_size, first, n_chunks, f...  58.5 us
    pallas_call x1, Pallas kernels, per_device(): pl.pallas_call(functools.partial(tail_kernel, n_dev, full_width), out_sha...  1.63 us

profile of v2, /device:TPU:0, one launch (start us, length us, event | category | flops | bytes accessed | tf_op | source)
XLA Modules:
  0.0 60.8 jit_solution(17683191610811773091)
XLA Ops:
  0.6 58.5 %shard_map.94 = (f32[16,31360]{1,0:T(8,128)S(1)}, f32[8,16,128]{2,1,0:T(8,128)S(1)}, f32[16,256]{1,0:T(8,128)S(1)}, f32[2,256]{1,0:T(2,128)S(1)}) custom-call(bf16[16,256]{1,0:T(8,128)(2,1)} %hid_hbm.1, f32[1,256]{1,0:T(1,128)} %bitcast.6, f32[1,256]{1,0:T(1,128)} %bitcast.7, bf16[125440,256]{1,0:T(8,128)(2,1)} %table_ref.1, s32[1,16]{1,0:T(1,128)} %bitcast.10, ...), custom_call_target="tpu_custom_call" | custom-call | tf_op jit(solution)/shard_map/pallas_call | solution.py:326
  59.1 1.6 %shard_map.95 = (f32[16,31360]{1,0:T(8,128)}, f32[1,16]{1,0:T(1,128)}, bf16[16,256]{1,0:T(8,128)(2,1)}) custom-call(f32[16,31360]{1,0:T(8,128)S(1)} %get-tuple-element.10.z_ref, f32[8,16,128]{2,1,0:T(8,128)S(1)} %get-tuple-element.11.sums_ref, f32[16,256]{1,0:T(8,128)S(1)} %get-tuple-element.12.rows_ref, f32[2,256]{1,0:T(2,128)S(1)} %get-tuple-element.13.affine_ref), custom_call_target="tpu_custom_call" | custom-call | tf_op jit(solution)/shard_map/pallas_call | solution.py:375

commit v3 on v2

v3 whole, which is shorter than its diff:
```python
import functools

import jax
import jax.numpy as jnp
from jax import lax
from jax.experimental import pallas as pl
from jax.experimental.pallas import tpu as pltpu
from jax.sharding import PartitionSpec as P

NORM_EPS = 1e-5
MESH = pl.DeviceIdType.MESH
LANES = 128
SUBLANES = 8
CHUNK = 1792
SMALL = (640, 1024, 1024)
SLOTS = 4
TAKES = 4
OUT_PARTS = 7


def row_sums(rows_f32):
    return jnp.sum(rows_f32, axis=1, keepdims=True), jnp.sum(rows_f32 * rows_f32, axis=1, keepdims=True)


def pack_lanes(columns):
    halves = [c[i * SUBLANES : (i + 1) * SUBLANES] for c in columns for i in range(2)]
    shape = (SUBLANES, LANES)
    lane = lax.broadcasted_iota(jnp.int32, shape, 1)
    span = LANES // len(halves)
    packed = jnp.broadcast_to(halves[0], shape)
    for i, column in enumerate(halves[1:], 1):
        packed = jnp.where(lane >= i * span, jnp.broadcast_to(column, shape), packed)
    return packed


def unpack_lanes(packed, i, n_columns):
    span = LANES // (2 * n_columns)
    at = 2 * i * span
    return jnp.concatenate([packed[:, at : at + 1], packed[:, at + span : at + span + 1]], axis=0)


def apply_norm(rows_f32, sums, squares, gain, bias, full_width):
    mean = sums / full_width
    var = squares / full_width - mean * mean
    scaled = (rows_f32 - mean) * lax.rsqrt(var + NORM_EPS)
    return (scaled * gain + bias).astype(jnp.bfloat16)


def main_kernel(
    vp_size, sizes, shared, full_width,
    hid_hbm, g1_hbm, b1_hbm, table_ref, tok_hbm, g2_hbm, b2_hbm,
    z_ref, sums_ref, rows_ref, affine_ref,
    hid_ref, g1_ref, b1_ref, tok_ref, tab, xn, push, give, take, land, land_diag, st, row_own, row_in, fs,
    in_sem, tab_sem, give_sem, take_sem, push_sem, land_sem, diag_sem,
    st_ssem, st_rsem, row_ssem, row_rsem, fs_ssem, fs_rsem,
):
    v = lax.axis_index("vp")
    t = lax.axis_index("tp")
    n_dev = vp_size * 4
    me = v * 4 + t
    core = t % 2
    chip = t // 2
    sib = chip * 2 + 1 - core
    across = (1 - chip) * 2 + core
    diag = (1 - chip) * 2 + 1 - core
    n_rows, block = z_ref.shape
    n_small = len(SMALL)
    n_steps = len(sizes)

    barrier = pltpu.get_barrier_semaphore()
    for d in range(1, n_dev):
        other = (me + d) % n_dev
        pl.semaphore_signal(barrier, inc=1, device_id={"vp": other // 4, "tp": other % 4}, device_id_type=MESH)

    def wait_sends(ref, sem):
        pltpu.make_async_remote_copy(
            ref, ref, sem, st_rsem.at[0], device_id={"tp": sib}, device_id_type=MESH
        ).wait_send()

    def wait_arrivals(ref, sem):
        pltpu.make_async_remote_copy(
            ref, ref, st_ssem.at[0], sem, device_id={"tp": sib}, device_id_type=MESH
        ).wait_recv()

    small = [
        pltpu.make_async_copy(src, dst, in_sem.at[i])
        for i, (src, dst) in enumerate((
            (hid_hbm, hid_ref), (g1_hbm, g1_ref), (b1_hbm, b1_ref), (tok_hbm, tok_ref),
            (g2_hbm, affine_ref.at[pl.ds(0, 1)]), (b2_hbm, affine_ref.at[pl.ds(1, 1)]),
        ))
    ]
    for copy in small:
        copy.start()

    def columns(step):
        if isinstance(step, int):
            return pl.ds(sum(sizes[:step]), sizes[step])
        return pl.ds(pl.multiple_of(sum(sizes[:n_small]) + (step - n_small) * CHUNK, LANES), CHUNK)

    def table_rows(phase, step, part):
        owner_chip = (1 - chip) if phase == 0 else chip
        owner_core = (1 - core) if part == 0 else core
        where = columns(step)
        return pl.ds(pl.multiple_of((owner_chip * 2 + owner_core) * block + where.start, LANES), where.size)

    def table_copy(phase, step, part):
        slot = (phase * n_steps + step) % SLOTS
        where = table_rows(phase, step, part)
        return pltpu.make_async_copy(
            table_ref.at[where, :], tab.at[slot, part, pl.ds(0, where.size)], tab_sem.at[slot, part]
        )

    def prefetch(phase, step):
        for part in range(2):
            table_copy(phase, step, part).start()

    for s in range(SLOTS):
        prefetch(0, s)

    small[0].wait()
    hid = hid_ref[...].astype(jnp.float32)
    st[t] = pack_lanes(row_sums(hid))
    pl.semaphore_wait(barrier, n_dev - 1)

    for target in (across, diag, sib):
        copy = pltpu.make_async_remote_copy(
            st.at[t], st.at[t], st_ssem.at[0], st_rsem.at[0], device_id={"tp": target}, device_id_type=MESH
        )
        copy.start()

    for copy in small[1:]:
        copy.wait()
    square = (n_rows, n_rows)
    on_diag = lax.broadcasted_iota(jnp.int32, square, 0) == lax.broadcasted_iota(jnp.int32, square, 1)
    tok_f32 = jnp.broadcast_to(tok_ref[...].astype(jnp.float32), square)
    tok_col = jnp.sum(jnp.where(on_diag, tok_f32, 0.0), axis=1, keepdims=True).astype(jnp.int32)
    tok_col = tok_col - v * (4 * block)
    row_own[...] = jnp.zeros_like(row_own)

    wait_arrivals(st.at[pl.ds(0, 3)], st_rsem.at[0])
    total = st[0] + st[1] + st[2] + st[3]
    xn[...] = apply_norm(
        hid, unpack_lanes(total, 0, 2), unpack_lanes(total, 1, 2), g1_ref[...], b1_ref[...], full_width
    )

    def give_copy(phase, step):
        where = columns(step)
        return pltpu.make_async_remote_copy(
            give.at[phase, :, where], take.at[phase, :, where], give_sem.at[0],
            take_sem.at[(phase * n_steps + step) % TAKES], device_id={"tp": sib}, device_id_type=MESH,
        )

    def push_copy(step, sem):
        where = columns(step)
        return pltpu.make_async_remote_copy(
            push.at[:, where], land.at[:, where], push_sem.at[0], land_sem.at[sem],
            device_id={"tp": across}, device_id_type=MESH,
        )

    def diag_copy():
        return pltpu.make_async_remote_copy(
            give.at[0, :, columns(0)], land_diag, give_sem.at[0], diag_sem.at[0],
            device_id={"tp": diag}, device_id_type=MESH,
        )

    def combine(phase, step, sem=None):
        where = columns(step)
        give_copy(phase, step).wait_recv()
        own = push if phase == 0 else z_ref
        own[:, where] = own[:, where] + take[phase, :, where]
        if phase == 0:
            push_copy(step, sem).start()

    def produce(phase, step, select=True):
        where = columns(step)
        slot = (phase * n_steps + step) % SLOTS
        for part in range(2):
            table_copy(phase, step, part).wait()
            vals = lax.dot_general(
                xn[...], tab[slot, part, 0 : where.size, :], (((1,), (1,)), ((), ())), preferred_element_type=jnp.float32
            )
            if part == 0:
                give[phase, :, where] = vals
            elif phase == 0:
                push[:, where] = vals
            else:
                z_ref[:, where] = vals
            if select:
                select_part(phase, step, part)
            if part == 0 and phase == 0 and isinstance(step, int) and step == 0:
                diag_copy().start()
            elif part == 0:
                give_copy(phase, step).start()

    def select_part(phase, step, part):
        where = table_rows(phase, step, part)
        slot = (phase * n_steps + step) % SLOTS
        hit = lax.broadcasted_iota(jnp.int32, (n_rows, where.size), 1) == tok_col - where.start
        ones = jnp.where(hit, 1.0, 0.0).astype(jnp.bfloat16)
        row_own[...] = row_own[...] + jnp.dot(
            ones, tab[slot, part, 0 : where.size, :], preferred_element_type=jnp.float32
        )

    produce(0, 0, select=False)
    push_copy(0, 0).start()
    produce(0, 1, select=False)
    produce(0, 2, select=False)

    def early_rows():
        for step in range(3):
            for part in range(2):
                select_part(0, step, part)

    pl.when(core == 1)(early_rows)
    combine(0, 1, 1)
    pl.when(core == 0)(early_rows)
    for step in range(3):
        prefetch(0, SLOTS + step)

    def far_step(step, carry):
        produce(0, step)
        combine(0, step - 1, 1)
        prefetch(0, step + SLOTS)
        return carry

    far_step(n_small, 0)
    lax.fori_loop(n_small + 1, n_steps - SLOTS, far_step, 0)
    for step in range(n_steps - SLOTS, n_steps):
        produce(0, step)
        combine(0, step - 1, max(step - 1 - shared, 0) + 1)
        prefetch(1, step + SLOTS - n_steps)

    for step in range(n_small + 1):
        produce(1, step)
        combine(0, n_steps - 1, n_steps - shared) if step == 0 else combine(1, step - 1)
        prefetch(1, SLOTS + step)

    def near_step(step, carry):
        produce(1, step)
        combine(1, step - 1)

        @pl.when(step + SLOTS < n_steps)
        def _():
            prefetch(1, step + SLOTS)

        return carry

    lax.fori_loop(n_small + 1, n_steps, near_step, 0)

    row_copies = []
    for d in range(1, vp_size):
        copy = pltpu.make_async_remote_copy(
            row_own, row_in.at[d - 1], row_ssem.at[d - 1], row_rsem.at[d - 1],
            device_id={"vp": (v + d) % vp_size}, device_id_type=MESH,
        )
        copy.start()
        row_copies.append(copy)
    combine(1, n_steps - 1)
    own_sums, own_squares = row_sums(row_own[...])

    def finish(step, carry, own_sem=False):
        where = columns(step)
        top, acc = carry
        if own_sem:
            push_copy(step, step - shared + 1).wait_recv()
        vals = z_ref[:, where] + land[:, where]
        if isinstance(step, int) and step == 0:
            vals = vals + land_diag[...]
        z_ref[:, where] = vals
        tiles = [vals[:, i * LANES : (i + 1) * LANES] for i in range(where.size // LANES)]
        new_top = functools.reduce(jnp.maximum, tiles, top)
        acc = acc * jnp.exp(top - new_top)
        for tile in tiles:
            acc = acc + jnp.exp(tile - new_top)
        return new_top, acc

    state = (jnp.full((n_rows, LANES), -jnp.inf, jnp.float32), jnp.zeros((n_rows, LANES), jnp.float32))
    push_copy(0, 0).wait_recv()
    diag_copy().wait_recv()
    together = land.at[:, pl.ds(sizes[0], sum(sizes[1 : shared + 1]))]
    wait_arrivals(together, land_sem.at[1])
    for step in range(n_small):
        state = finish(step, state)
    state = lax.fori_loop(n_small, shared + 1, finish, state)
    top, acc = lax.fori_loop(shared + 1, n_steps, functools.partial(finish, own_sem=True), state)
    row_top = jnp.max(top, axis=1, keepdims=True)
    row_sum = jnp.sum(acc * jnp.exp(top - row_top), axis=1, keepdims=True)
    fs[me] = pack_lanes((row_top, row_sum, own_sums, own_squares))
    for d in range(1, n_dev):
        other = (me + d) % n_dev
        copy = pltpu.make_async_remote_copy(
            fs.at[me], fs.at[me], fs_ssem.at[0], fs_rsem.at[0],
            device_id={"vp": other // 4, "tp": other % 4}, device_id_type=MESH,
        )
        copy.start()

    rows = row_own[...]
    for d in range(1, vp_size):
        row_copies[d - 1].wait_recv()
        rows = rows + row_in[d - 1]
    rows_ref[...] = rows
    for copy in row_copies:
        copy.wait_send()
    wait_sends(st.at[pl.ds(0, 3)], st_ssem.at[0])
    wait_sends(give, give_sem.at[0])
    wait_sends(push, push_sem.at[0])
    wait_arrivals(fs.at[pl.ds(0, n_dev - 1)], fs_rsem.at[0])
    wait_sends(fs.at[pl.ds(0, n_dev - 1)], fs_ssem.at[0])
    sums_ref[...] = fs[...]


def tail_kernel(
    n_dev, full_width, z_ref, sums_ref, rows_ref, affine_ref, out_hbm, ls_hbm, nxt_hbm, out, ls, nxt, sem
):
    packed = [sums_ref[i] for i in range(n_dev)]
    tops = [unpack_lanes(p, 0, 4) for p in packed]
    all_top = functools.reduce(jnp.maximum, tops)
    all_sum = functools.reduce(jnp.add, [unpack_lanes(p, 1, 4) * jnp.exp(m - all_top) for p, m in zip(packed, tops)])
    log_sum = all_top + jnp.log(all_sum)
    n_rows, block = out.shape
    part = block // OUT_PARTS
    for i in range(OUT_PARTS):
        columns = pl.ds(i * part, part)
        out[:, columns] = z_ref[:, columns] - log_sum
        pltpu.make_async_copy(out.at[:, columns], out_hbm.at[:, columns], sem.at[0]).start()
    square = (n_rows, n_rows)
    on_diag = lax.broadcasted_iota(jnp.int32, square, 0) == lax.broadcasted_iota(jnp.int32, square, 1)
    ls[...] = jnp.sum(jnp.where(on_diag, jnp.broadcast_to(log_sum, square), 0.0), axis=0, keepdims=True)
    ls_copy = pltpu.make_async_copy(ls, ls_hbm, sem.at[1])
    ls_copy.start()
    sums = functools.reduce(jnp.add, [unpack_lanes(p, 2, 4) for p in packed])
    squares = functools.reduce(jnp.add, [unpack_lanes(p, 3, 4) for p in packed])
    nxt[...] = apply_norm(rows_ref[...], sums, squares, affine_ref[0:1, :], affine_ref[1:2, :], full_width)
    nxt_copy = pltpu.make_async_copy(nxt, nxt_hbm, sem.at[2])
    nxt_copy.start()
    pltpu.make_async_copy(out, out_hbm, sem.at[0]).wait()
    ls_copy.wait()
    nxt_copy.wait()


def solution(mesh):
    tp_size = mesh.shape["tp"]
    vp_size = mesh.shape["vp"]
    n_dev = tp_size * vp_size

    def per_device(hidden, lnf_gain, lnf_bias, emb_table, next_tok, eln_gain, eln_bias):
        n_rows, width = hidden.shape
        full_width = width * tp_size
        block = emb_table.shape[0] // tp_size
        sizes = SMALL + (CHUNK,) * ((block - sum(SMALL)) // CHUNK)
        assert sum(sizes) == block
        shared = len(sizes) - SLOTS - 1

        dma = pltpu.SemaphoreType.DMA
        f32 = jnp.float32
        hbm = pl.BlockSpec(memory_space=pltpu.HBM)
        vmem = pl.BlockSpec(memory_space=pltpu.VMEM)
        row = lambda a: a.reshape(1, a.shape[0])
        z, sums, rows, affine = pl.pallas_call(
            functools.partial(main_kernel, vp_size, sizes, shared, full_width),
            out_shape=(
                pltpu.VMEM((n_rows, block), f32),
                pltpu.VMEM((n_dev, SUBLANES, LANES), f32),
                pltpu.VMEM((n_rows, width), f32),
                pltpu.VMEM((2, width), f32),
            ),
            in_specs=[hbm] * 7,
            out_specs=(vmem,) * 4,
            scratch_shapes=[
                pltpu.VMEM((n_rows, width), jnp.bfloat16),
                pltpu.VMEM((1, width), f32),
                pltpu.VMEM((1, width), f32),
                pltpu.VMEM((1, n_rows), jnp.int32),
                pltpu.VMEM((SLOTS, 2, CHUNK, width), jnp.bfloat16),
                pltpu.VMEM((n_rows, width), jnp.bfloat16),
                pltpu.VMEM((n_rows, block), f32),
                pltpu.VMEM((2, n_rows, block), f32),
                pltpu.VMEM((2, n_rows, block), f32),
                pltpu.VMEM((n_rows, block), f32),
                pltpu.VMEM((n_rows, SMALL[0]), f32),
                pltpu.VMEM((tp_size, SUBLANES, LANES), f32),
                pltpu.VMEM((n_rows, width), f32),
                pltpu.VMEM((vp_size - 1, n_rows, width), f32),
                pltpu.VMEM((n_dev, SUBLANES, LANES), f32),
                dma((6,)),
                dma((SLOTS, 2)),
                dma((1,)),
                dma((TAKES,)),
                dma((1,)),
                dma((len(sizes) - shared + 1,)),
                dma((1,)),
                dma((1,)),
                dma((1,)),
                dma((vp_size - 1,)),
                dma((vp_size - 1,)),
                dma((1,)),
                dma((1,)),
            ],
            compiler_params=pltpu.CompilerParams(
                collective_id=0, has_side_effects=True, vmem_limit_bytes=40 * 2**20
            ),
        )(*(
            pltpu.with_memory_space_constraint(a, pltpu.HBM)
            for a in (hidden, row(lnf_gain), row(lnf_bias), emb_table, row(next_tok), row(eln_gain), row(eln_bias))
        ))
        logprobs, log_sum, next_in = pl.pallas_call(
            functools.partial(tail_kernel, n_dev, full_width),
            out_shape=(
                jax.ShapeDtypeStruct((n_rows, block), f32),
                jax.ShapeDtypeStruct((1, n_rows), f32),
                jax.ShapeDtypeStruct((n_rows, width), jnp.bfloat16),
            ),
            in_specs=[vmem] * 4,
            out_specs=(pl.BlockSpec(memory_space=pl.ANY),) * 3,
            scratch_shapes=[
                pltpu.VMEM((n_rows, block), f32),
                pltpu.VMEM((1, n_rows), f32),
                pltpu.VMEM((n_rows, width), jnp.bfloat16),
                dma((3,)),
            ],
            compiler_params=pltpu.CompilerParams(vmem_limit_bytes=12 * 2**20),
        )(*(pltpu.with_memory_space_constraint(a, pltpu.VMEM) for a in (z, sums, rows, affine)))
        return logprobs, log_sum.reshape(n_rows), next_in

    return jax.shard_map(
        per_device,
        mesh=mesh,
        in_specs=(P("dp", "tp"), P("tp"), P("tp"), P("vp", "tp"), P("dp"), P("tp"), P("tp")),
        out_specs=(P("dp", ("vp", "tp")), P("dp"), P("dp", "tp")),
        check_vma=False,
    )
```

time: 60.9 us -> 58.8 us (0.966)
  Pallas kernels: 60.1 us -> 58 us
    pallas_call x1, Pallas kernels: 58.5 us -> 56.4 us  [per_device(): pl.pallas_call(functools.partial(main_kernel, vp_size, sizes, shared, ful...]
where the time goes in v3:
time: 58.8 us; the launch traced here: 58.7 us
  Pallas kernels  58 us (99%)
  between operations  0.64 us (1%)
    pallas_call x1, Pallas kernels, per_device(): pl.pallas_call(functools.partial(main_kernel, vp_size, sizes, shared, ful...  56.4 us
    pallas_call x1, Pallas kernels, per_device(): pl.pallas_call(functools.partial(tail_kernel, n_dev, full_width), out_sha...  1.63 us

profile of v3, /device:TPU:0, one launch (start us, length us, event | category | flops | bytes accessed | tf_op | source)
XLA Modules:
  0.0 58.7 jit_solution(9013686545918494857)
XLA Ops:
  0.6 56.4 %shard_map.94 = (f32[16,31360]{1,0:T(8,128)S(1)}, f32[8,8,128]{2,1,0:T(8,128)S(1)}, f32[16,256]{1,0:T(8,128)S(1)}, f32[2,256]{1,0:T(2,128)S(1)}) custom-call(bf16[16,256]{1,0:T(8,128)(2,1)} %hid_hbm.1, f32[1,256]{1,0:T(1,128)} %bitcast.6, f32[1,256]{1,0:T(1,128)} %bitcast.7, bf16[125440,256]{1,0:T(8,128)(2,1)} %table_ref.1, s32[1,16]{1,0:T(1,128)} %bitcast.10, ...), custom_call_target="tpu_custom_call" | custom-call | tf_op jit(solution)/shard_map/pallas_call | solution.py:359
  57.0 1.6 %shard_map.95 = (f32[16,31360]{1,0:T(8,128)}, f32[1,16]{1,0:T(1,128)}, bf16[16,256]{1,0:T(8,128)(2,1)}) custom-call(f32[16,31360]{1,0:T(8,128)S(1)} %get-tuple-element.10.z_ref, f32[8,8,128]{2,1,0:T(8,128)S(1)} %get-tuple-element.11.sums_ref, f32[16,256]{1,0:T(8,128)S(1)} %get-tuple-element.12.rows_ref, f32[2,256]{1,0:T(2,128)S(1)} %get-tuple-element.13.affine_ref), custom_call_target="tpu_custom_call" | custom-call | tf_op jit(solution)/shard_map/pallas_call | solution.py:406

commit v4 on v3

--- a/solution.py
+++ b/solution.py
@@ -114,10 +114,9 @@
         for part in range(2):
             table_copy(phase, step, part).start()
 
+    small[0].wait()
     for s in range(SLOTS):
         prefetch(0, s)
-
-    small[0].wait()
     hid = hid_ref[...].astype(jnp.float32)
     st[t] = pack_lanes(row_sums(hid))
     pl.semaphore_wait(barrier, n_dev - 1)
@@ -163,12 +162,12 @@
             device_id={"tp": diag}, device_id_type=MESH,
         )
 
-    def combine(phase, step, sem=None):
+    def combine(phase, step, sem=None, send=True):
         where = columns(step)
         give_copy(phase, step).wait_recv()
         own = push if phase == 0 else z_ref
         own[:, where] = own[:, where] + take[phase, :, where]
-        if phase == 0:
+        if phase == 0 and send:
             push_copy(step, sem).start()
 
     def produce(phase, step, select=True):
@@ -219,7 +218,17 @@
 
     def far_step(step, carry):
         produce(0, step)
-        combine(0, step - 1, 1)
+        combine(0, step - 1, 1, send=False)
+        hold = (core == 1) & (step >= 4) & (step < 6)
+
+        @pl.when(jnp.logical_not(hold))
+        def _():
+            push_copy(step - 1, 1).start()
+
+        @pl.when((core == 1) & (step == 6))
+        def _():
+            push_copy(step - 3, 1).start()
+            push_copy(step - 2, 1).start()
         prefetch(0, step + SLOTS)
         return carry
 
@@ -313,16 +322,20 @@
     n_dev, full_width, z_ref, sums_ref, rows_ref, affine_ref, out_hbm, ls_hbm, nxt_hbm, out, ls, nxt, sem
 ):
     packed = [sums_ref[i] for i in range(n_dev)]
-    tops = [unpack_lanes(p, 0, 4) for p in packed]
+    n_rows, block = out.shape
+    wide = lambda p, i: jnp.broadcast_to(unpack_lanes(p, i, 4), (n_rows, LANES))
+    tops = [wide(p, 0) for p in packed]
     all_top = functools.reduce(jnp.maximum, tops)
-    all_sum = functools.reduce(jnp.add, [unpack_lanes(p, 1, 4) * jnp.exp(m - all_top) for p, m in zip(packed, tops)])
-    log_sum = all_top + jnp.log(all_sum)
-    n_rows, block = out.shape
+    all_sum = functools.reduce(jnp.add, [wide(p, 1) * jnp.exp(m - all_top) for p, m in zip(packed, tops)])
+    wide_log_sum = all_top + jnp.log(all_sum)
     part = block // OUT_PARTS
     for i in range(OUT_PARTS):
+        for k in range(part // LANES):
+            tile = pl.ds(i * part + k * LANES, LANES)
+            out[:, tile] = z_ref[:, tile] - wide_log_sum
         columns = pl.ds(i * part, part)
-        out[:, columns] = z_ref[:, columns] - log_sum
         pltpu.make_async_copy(out.at[:, columns], out_hbm.at[:, columns], sem.at[0]).start()
+    log_sum = wide_log_sum[:, 0:1]
     square = (n_rows, n_rows)
     on_diag = lax.broadcasted_iota(jnp.int32, square, 0) == lax.broadcasted_iota(jnp.int32, square, 1)
     ls[...] = jnp.sum(jnp.where(on_diag, jnp.broadcast_to(log_sum, square), 0.0), axis=0, keepdims=True)
@@ -349,7 +362,7 @@
         block = emb_table.shape[0] // tp_size
         sizes = SMALL + (CHUNK,) * ((block - sum(SMALL)) // CHUNK)
         assert sum(sizes) == block
-        shared = len(sizes) - SLOTS - 1
+        shared = len(sizes) - 3
 
         dma = pltpu.SemaphoreType.DMA
         f32 = jnp.float32

time: 58.8 us -> 57.6 us (0.980)
  Pallas kernels: 58 us -> 56.8 us
    pallas_call x1, Pallas kernels: 56.4 us -> 55.3 us  [per_device(): pl.pallas_call(functools.partial(main_kernel, vp_size, sizes, shared, ful...]
where the time goes in v4:
time: 57.6 us; the launch traced here: 57.4 us
  Pallas kernels  56.8 us (99%)
  between operations  0.64 us (1%)
    pallas_call x1, Pallas kernels, per_device(): pl.pallas_call(functools.partial(main_kernel, vp_size, sizes, shared, ful...  55.3 us
    pallas_call x1, Pallas kernels, per_device(): pl.pallas_call(functools.partial(tail_kernel, n_dev, full_width), out_sha...  1.51 us

profile of v4, /device:TPU:0, one launch (start us, length us, event | category | flops | bytes accessed | tf_op | source)
XLA Modules:
  0.0 57.4 jit_solution(6593734389265142288)
XLA Ops:
  0.6 55.3 %shard_map.94 = (f32[16,31360]{1,0:T(8,128)S(1)}, f32[8,8,128]{2,1,0:T(8,128)S(1)}, f32[16,256]{1,0:T(8,128)S(1)}, f32[2,256]{1,0:T(2,128)S(1)}) custom-call(bf16[16,256]{1,0:T(8,128)(2,1)} %hid_hbm.1, f32[1,256]{1,0:T(1,128)} %bitcast.6, f32[1,256]{1,0:T(1,128)} %bitcast.7, bf16[125440,256]{1,0:T(8,128)(2,1)} %table_ref.1, s32[1,16]{1,0:T(1,128)} %bitcast.10, ...), custom_call_target="tpu_custom_call" | custom-call | tf_op jit(solution)/shard_map/pallas_call | solution.py:372
  55.9 1.5 %shard_map.95 = (f32[16,31360]{1,0:T(8,128)}, f32[1,16]{1,0:T(1,128)}, bf16[16,256]{1,0:T(8,128)(2,1)}) custom-call(f32[16,31360]{1,0:T(8,128)S(1)} %get-tuple-element.10.z_ref, f32[8,8,128]{2,1,0:T(8,128)S(1)} %get-tuple-element.11.sums_ref, f32[16,256]{1,0:T(8,128)S(1)} %get-tuple-element.12.rows_ref, f32[2,256]{1,0:T(2,128)S(1)} %get-tuple-element.13.affine_ref), custom_call_target="tpu_custom_call" | custom-call | tf_op jit(solution)/shard_map/pallas_call | solution.py:419

commit v5 on v4

--- a/solution.py
+++ b/solution.py
@@ -15,7 +15,7 @@
 SMALL = (640, 1024, 1024)
 SLOTS = 4
 TAKES = 4
-OUT_PARTS = 7
+OUT_PARTS = 35
 
 
 def row_sums(rows_f32):
@@ -67,6 +67,8 @@
     n_small = len(SMALL)
     n_steps = len(sizes)
 
+    hid_copy = pltpu.make_async_copy(hid_hbm, hid_ref, in_sem.at[0])
+    hid_copy.start()
     barrier = pltpu.get_barrier_semaphore()
     for d in range(1, n_dev):
         other = (me + d) % n_dev
@@ -83,9 +85,9 @@
         ).wait_recv()
 
     small = [
-        pltpu.make_async_copy(src, dst, in_sem.at[i])
+        pltpu.make_async_copy(src, dst, in_sem.at[i + 1])
         for i, (src, dst) in enumerate((
-            (hid_hbm, hid_ref), (g1_hbm, g1_ref), (b1_hbm, b1_ref), (tok_hbm, tok_ref),
+            (g1_hbm, g1_ref), (b1_hbm, b1_ref), (tok_hbm, tok_ref),
             (g2_hbm, affine_ref.at[pl.ds(0, 1)]), (b2_hbm, affine_ref.at[pl.ds(1, 1)]),
         ))
     ]
@@ -114,7 +116,7 @@
         for part in range(2):
             table_copy(phase, step, part).start()
 
-    small[0].wait()
+    hid_copy.wait()
     for s in range(SLOTS):
         prefetch(0, s)
     hid = hid_ref[...].astype(jnp.float32)
@@ -127,7 +129,7 @@
         )
         copy.start()
 
-    for copy in small[1:]:
+    for copy in small:
         copy.wait()
     square = (n_rows, n_rows)
     on_diag = lax.broadcasted_iota(jnp.int32, square, 0) == lax.broadcasted_iota(jnp.int32, square, 1)
@@ -138,9 +140,8 @@
 
     wait_arrivals(st.at[pl.ds(0, 3)], st_rsem.at[0])
     total = st[0] + st[1] + st[2] + st[3]
-    xn[...] = apply_norm(
-        hid, unpack_lanes(total, 0, 2), unpack_lanes(total, 1, 2), g1_ref[...], b1_ref[...], full_width
-    )
+    wide = lambda i: jnp.broadcast_to(unpack_lanes(total, i, 2), hid.shape)
+    xn[...] = apply_norm(hid, wide(0), wide(1), g1_ref[...], b1_ref[...], full_width)
 
     def give_copy(phase, step):
         where = columns(step)

time: 57.6 us -> 57.4 us (level)
  no operation moved by 1% of the time
where the time goes in v5:
time: 57.4 us; the launch traced here: 57.2 us
  Pallas kernels  56.6 us (99%)
  between operations  0.64 us (1%)
    pallas_call x1, Pallas kernels, per_device(): pl.pallas_call(functools.partial(main_kernel, vp_size, sizes, shared, ful...  55.1 us
    pallas_call x1, Pallas kernels, per_device(): pl.pallas_call(functools.partial(tail_kernel, n_dev, full_width), out_sha...  1.46 us

profile of v5, /device:TPU:0, one launch (start us, length us, event | category | flops | bytes accessed | tf_op | source)
XLA Modules:
  0.0 57.2 jit_solution(14696915014508414955)
XLA Ops:
  0.6 55.1 %shard_map.94 = (f32[16,31360]{1,0:T(8,128)S(1)}, f32[8,8,128]{2,1,0:T(8,128)S(1)}, f32[16,256]{1,0:T(8,128)S(1)}, f32[2,256]{1,0:T(2,128)S(1)}) custom-call(bf16[16,256]{1,0:T(8,128)(2,1)} %hid_hbm.1, f32[1,256]{1,0:T(1,128)} %bitcast.6, f32[1,256]{1,0:T(1,128)} %bitcast.7, bf16[125440,256]{1,0:T(8,128)(2,1)} %table_ref.1, s32[1,16]{1,0:T(1,128)} %bitcast.10, ...), custom_call_target="tpu_custom_call" | custom-call | tf_op jit(solution)/shard_map/pallas_call | solution.py:373
  55.7 1.5 %shard_map.95 = (f32[16,31360]{1,0:T(8,128)}, f32[1,16]{1,0:T(1,128)}, bf16[16,256]{1,0:T(8,128)(2,1)}) custom-call(f32[16,31360]{1,0:T(8,128)S(1)} %get-tuple-element.10.z_ref, f32[8,8,128]{2,1,0:T(8,128)S(1)} %get-tuple-element.11.sums_ref, f32[16,256]{1,0:T(8,128)S(1)} %get-tuple-element.12.rows_ref, f32[2,256]{1,0:T(2,128)S(1)} %get-tuple-element.13.affine_ref), custom_call_target="tpu_custom_call" | custom-call | tf_op jit(solution)/shard_map/pallas_call | solution.py:420

commit v6 on v5

--- a/solution.py
+++ b/solution.py
@@ -12,7 +12,7 @@
 LANES = 128
 SUBLANES = 8
 CHUNK = 1792
-SMALL = (640, 1024, 1024)
+SMALL = (512, 512, 1664)
 SLOTS = 4
 TAKES = 4
 OUT_PARTS = 35
@@ -171,25 +171,25 @@
         if phase == 0 and send:
             push_copy(step, sem).start()
 
-    def produce(phase, step, select=True):
+    def logits_part(phase, step, part):
         where = columns(step)
         slot = (phase * n_steps + step) % SLOTS
+        table_copy(phase, step, part).wait()
+        vals = lax.dot_general(
+            xn[...], tab[slot, part, 0 : where.size, :], (((1,), (1,)), ((), ())), preferred_element_type=jnp.float32
+        )
+        if part == 0:
+            give[phase, :, where] = vals
+        elif phase == 0:
+            push[:, where] = vals
+        else:
+            z_ref[:, where] = vals
+
+    def produce(phase, step):
         for part in range(2):
-            table_copy(phase, step, part).wait()
-            vals = lax.dot_general(
-                xn[...], tab[slot, part, 0 : where.size, :], (((1,), (1,)), ((), ())), preferred_element_type=jnp.float32
-            )
+            logits_part(phase, step, part)
+            select_part(phase, step, part)
             if part == 0:
-                give[phase, :, where] = vals
-            elif phase == 0:
-                push[:, where] = vals
-            else:
-                z_ref[:, where] = vals
-            if select:
-                select_part(phase, step, part)
-            if part == 0 and phase == 0 and isinstance(step, int) and step == 0:
-                diag_copy().start()
-            elif part == 0:
                 give_copy(phase, step).start()
 
     def select_part(phase, step, part):
@@ -201,39 +201,58 @@
             ones, tab[slot, part, 0 : where.size, :], preferred_element_type=jnp.float32
         )
 
-    produce(0, 0, select=False)
+    logits_part(0, 0, 0)
+    diag_copy().start()
+    logits_part(0, 1, 0)
+    give_copy(0, 1).start()
+    logits_part(0, 0, 1)
     push_copy(0, 0).start()
-    produce(0, 1, select=False)
-    produce(0, 2, select=False)
-
-    def early_rows():
-        for step in range(3):
+    logits_part(0, 1, 1)
+    logits_part(0, 2, 0)
+    give_copy(0, 2).start()
+    logits_part(0, 2, 1)
+
+    def early_rows(steps):
+        for step in steps:
             for part in range(2):
                 select_part(0, step, part)
-
-    pl.when(core == 1)(early_rows)
-    combine(0, 1, 1)
-    pl.when(core == 0)(early_rows)
-    for step in range(3):
-        prefetch(0, SLOTS + step)
+            prefetch(0, SLOTS + step)
+
+    @pl.when(core == 0)
+    def _():
+        combine(0, 1, 1)
+        early_rows((0, 1))
+        combine(0, 2, 1)
+        early_rows((2,))
+
+    @pl.when(core == 1)
+    def _():
+        early_rows((0, 1))
+        combine(0, 1, 1)
+        combine(0, 2, 1)
+        early_rows((2,))
+
+    produce(0, n_small)
+    prefetch(0, SLOTS + n_small)
 
     def far_step(step, carry):
         produce(0, step)
         combine(0, step - 1, 1, send=False)
-        hold = (core == 1) & (step >= 4) & (step < 6)
+        hold = (core == 1) & (step >= 5) & (step < 8)
 
         @pl.when(jnp.logical_not(hold))
         def _():
             push_copy(step - 1, 1).start()
 
-        @pl.when((core == 1) & (step == 6))
+        @pl.when((core == 1) & (step == 8))
         def _():
+            push_copy(step - 4, 1).start()
             push_copy(step - 3, 1).start()
             push_copy(step - 2, 1).start()
+
         prefetch(0, step + SLOTS)
         return carry
 
-    far_step(n_small, 0)
     lax.fori_loop(n_small + 1, n_steps - SLOTS, far_step, 0)
     for step in range(n_steps - SLOTS, n_steps):
         produce(0, step)
@@ -296,8 +315,8 @@
     row_top = jnp.max(top, axis=1, keepdims=True)
     row_sum = jnp.sum(acc * jnp.exp(top - row_top), axis=1, keepdims=True)
     fs[me] = pack_lanes((row_top, row_sum, own_sums, own_squares))
-    for d in range(1, n_dev):
-        other = (me + d) % n_dev
+    for d in range(n_dev - 1):
+        other = d + (d - me + n_dev) // n_dev
         copy = pltpu.make_async_remote_copy(
             fs.at[me], fs.at[me], fs_ssem.at[0], fs_rsem.at[0],
             device_id={"vp": other // 4, "tp": other % 4}, device_id_type=MESH,

time: 57.4 us -> 57.3 us (level)
  no operation moved by 1% of the time
where the time goes in v6:
time: 57.3 us; the launch traced here: 57.2 us
  Pallas kernels  56.5 us (99%)
  between operations  0.64 us (1%)
    pallas_call x1, Pallas kernels, per_device(): pl.pallas_call(functools.partial(main_kernel, vp_size, sizes, shared, ful...  55.1 us
    pallas_call x1, Pallas kernels, per_device(): pl.pallas_call(functools.partial(tail_kernel, n_dev, full_width), out_sha...  1.46 us

profile of v6, /device:TPU:0, one launch (start us, length us, event | category | flops | bytes accessed | tf_op | source)
XLA Modules:
  0.0 57.2 jit_solution(7282815581659259496)
XLA Ops:
  0.6 55.1 %shard_map.94 = (f32[16,31360]{1,0:T(8,128)S(1)}, f32[8,8,128]{2,1,0:T(8,128)S(1)}, f32[16,256]{1,0:T(8,128)S(1)}, f32[2,256]{1,0:T(2,128)S(1)}) custom-call(bf16[16,256]{1,0:T(8,128)(2,1)} %hid_hbm.1, f32[1,256]{1,0:T(1,128)} %bitcast.6, f32[1,256]{1,0:T(1,128)} %bitcast.7, bf16[125440,256]{1,0:T(8,128)(2,1)} %table_ref.1, s32[1,16]{1,0:T(1,128)} %bitcast.10, ...), custom_call_target="tpu_custom_call" | custom-call | tf_op jit(solution)/shard_map/pallas_call | solution.py:392
  55.7 1.5 %shard_map.95 = (f32[16,31360]{1,0:T(8,128)}, f32[1,16]{1,0:T(1,128)}, bf16[16,256]{1,0:T(8,128)(2,1)}) custom-call(f32[16,31360]{1,0:T(8,128)S(1)} %get-tuple-element.10.z_ref, f32[8,8,128]{2,1,0:T(8,128)S(1)} %get-tuple-element.11.sums_ref, f32[16,256]{1,0:T(8,128)S(1)} %get-tuple-element.12.rows_ref, f32[2,256]{1,0:T(2,128)S(1)} %get-tuple-element.13.affine_ref), custom_call_target="tpu_custom_call" | custom-call | tf_op jit(solution)/shard_map/pallas_call | solution.py:439

commit v7 on v6

--- a/solution.py
+++ b/solution.py
@@ -85,11 +85,11 @@
         ).wait_recv()
 
     small = [
-        pltpu.make_async_copy(src, dst, in_sem.at[i + 1])
-        for i, (src, dst) in enumerate((
+        pltpu.make_async_copy(src, dst, in_sem.at[1])
+        for src, dst in (
             (g1_hbm, g1_ref), (b1_hbm, b1_ref), (tok_hbm, tok_ref),
             (g2_hbm, affine_ref.at[pl.ds(0, 1)]), (b2_hbm, affine_ref.at[pl.ds(1, 1)]),
-        ))
+        )
     ]
     for copy in small:
         copy.start()
@@ -415,7 +415,7 @@
                 pltpu.VMEM((n_rows, width), f32),
                 pltpu.VMEM((vp_size - 1, n_rows, width), f32),
                 pltpu.VMEM((n_dev, SUBLANES, LANES), f32),
-                dma((6,)),
+                dma((2,)),
                 dma((SLOTS, 2)),
                 dma((1,)),
                 dma((TAKES,)),

time: 57.3 us -> 57.3 us (level)
  no operation moved by 1% of the time
where the time goes in v7:
time: 57.3 us; the launch traced here: 57.1 us
  Pallas kernels  56.5 us (99%)
  between operations  0.64 us (1%)
    pallas_call x1, Pallas kernels, per_device(): pl.pallas_call(functools.partial(main_kernel, vp_size, sizes, shared, ful...  55 us
    pallas_call x1, Pallas kernels, per_device(): pl.pallas_call(functools.partial(tail_kernel, n_dev, full_width), out_sha...  1.46 us

profile of v7, /device:TPU:0, one launch (start us, length us, event | category | flops | bytes accessed | tf_op | source)
XLA Modules:
  0.0 57.1 jit_solution(11419693022655447387)
XLA Ops:
  0.6 55.0 %shard_map.94 = (f32[16,31360]{1,0:T(8,128)S(1)}, f32[8,8,128]{2,1,0:T(8,128)S(1)}, f32[16,256]{1,0:T(8,128)S(1)}, f32[2,256]{1,0:T(2,128)S(1)}) custom-call(bf16[16,256]{1,0:T(8,128)(2,1)} %hid_hbm.1, f32[1,256]{1,0:T(1,128)} %bitcast.6, f32[1,256]{1,0:T(1,128)} %bitcast.7, bf16[125440,256]{1,0:T(8,128)(2,1)} %table_ref.1, s32[1,16]{1,0:T(1,128)} %bitcast.10, ...), custom_call_target="tpu_custom_call" | custom-call | tf_op jit(solution)/shard_map/pallas_call | solution.py:392
  55.7 1.5 %shard_map.95 = (f32[16,31360]{1,0:T(8,128)}, f32[1,16]{1,0:T(1,128)}, bf16[16,256]{1,0:T(8,128)(2,1)}) custom-call(f32[16,31360]{1,0:T(8,128)S(1)} %get-tuple-element.10.z_ref, f32[8,8,128]{2,1,0:T(8,128)S(1)} %get-tuple-element.11.sums_ref, f32[16,256]{1,0:T(8,128)S(1)} %get-tuple-element.12.rows_ref, f32[2,256]{1,0:T(2,128)S(1)} %get-tuple-element.13.affine_ref), custom_call_target="tpu_custom_call" | custom-call | tf_op jit(solution)/shard_map/pallas_call | solution.py:439
